TPU v7x, 32 devices: a whole 2x2x4 slice. The times are simulated.
32 devices in a mesh: grp: 2 (over y), zt: 4 (over x, core), xy: 4 (over z).
Axes of the slice: x: 2, y: 2, z: 4, core: 2. Of those that a mesh axis runs over, the one named last changes fastest.
Arguments:
- source: float32 [2, 2, 3, 8, 16, 128], P('grp', None, None, 'xy', 'zt'), may hold values from -6 to 6
- links: float32 [4, 2, 3, 3, 8, 16, 128], P('grp', None, None, None, 'xy', 'zt'), may hold values from -2 to 2
- shifts: float32 [12], replicated, may hold values from 0.01 to 0.5
- residues: float32 [12], replicated, may hold values from 0.05 to 0.5
- mass: float32 [1], replicated, may hold values from 0.1 to 0.5
Outputs:
- rational: float32 [2, 2, 3, 8, 16, 128], P('grp', None, None, 'xy', 'zt')
- action: float32 [1], replicated
All inputs are finite; a program needn't handle non-finite values.
Results may differ from a plain program's by a relative error of at most 0.0003.
Values sent between devices are 32-bit elements; how exact they have to be, the bound alone decides.
A program may use at most 64 MiB of HBM per device.

v0:
```python
import functools

import jax
import jax.numpy as jnp
from jax import lax
from jax.experimental import pallas as pl
from jax.experimental.pallas import tpu as pltpu
from jax.sharding import PartitionSpec as P

NY = 2
NZ = 64
ITERS = 8
PAIRS = 9
MAT = 2 * PAIRS
COMPS = 6


def roll(value, shift, axis):
    size = value.shape[axis]
    return pltpu.roll(value, shift % size, axis)


def kernel(
    dims, source_hbm, links_hbm, shifts_ref, residues_ref, mass_ref, out_ref, action_ref,
    lk, tfar, xfar, xtwo, sx, sx2, cs_ll, cs_hl, cs_lh, c_ll, c_hl, c_lh,
    gauge, dirn, resid, mid, shiftdirs, rpack, ws, wr, cs, cr, part, act,
    state, source_ref, links_ref, isem, lsend, lrecv, hsend, hrecv, psend, precv, asend, arecv,
):
    n_grp, n_zt, n_xy, cells_x, cells_t = dims
    lanes = NY * NZ
    n_all = n_zt * n_xy
    nshift = shifts_ref.shape[0]
    g = lax.axis_index("grp")
    zt = lax.axis_index("zt")
    xy = lax.axis_index("xy")
    me = zt * n_xy + xy
    me_all = g * n_all + me
    x_up, x_dn = lax.rem(xy + 1, n_xy), lax.rem(xy + n_xy - 1, n_xy)
    t_up, t_dn = lax.rem(zt + 1, n_zt), lax.rem(zt + n_zt - 1, n_zt)
    other = 1 - g

    def place(linear):
        inside = lax.rem(linear, n_all)
        return (linear // n_all, inside // n_xy, lax.rem(inside, n_xy))

    def each(count, fn):
        if count <= 32:
            for p in range(1, count):
                fn(p)
        else:
            def step(p, carry):
                fn(p)
                return carry
            lax.fori_loop(1, count, step, 0)

    def copy(src, dst, send, recv, device):
        return pltpu.make_async_remote_copy(
            src_ref=src, dst_ref=dst, send_sem=send, recv_sem=recv,
            device_id=device, device_id_type=pl.DeviceIdType.MESH,
        )

    barrier = pltpu.get_barrier_semaphore()

    def greet(p):
        pl.semaphore_signal(
            barrier, inc=1, device_id=place(lax.rem(me_all + p, n_grp * n_all)),
            device_id_type=pl.DeviceIdType.MESH,
        )

    fetch_links = pltpu.make_async_copy(links_hbm, links_ref, isem.at[0])
    fetch_source = pltpu.make_async_copy(source_hbm, source_ref, isem.at[1])
    fetch_links.start()
    fetch_source.start()
    each(n_grp * n_all, greet)
    fetch_links.wait()
    fetch_source.wait()

    sub = lax.broadcasted_iota(jnp.int32, (8, lanes), 0)
    lane = lax.broadcasted_iota(jnp.int32, (8, lanes), 1)
    zcoord = lax.rem(lane, NZ)
    ycoord = lane // NZ
    quarter = lanes // 4
    home = sub == lane // quarter
    own = (sub >= 2) & (sub < 2 + cells_t)
    first = sub < cells_t
    late = lax.rem(sub, cells_t) >= 2

    for d in range(2):
        for c in range(MAT):
            low, high = links_ref[c], links_ref[MAT + c]
            if d == 0:
                sx[0, pl.ds(g * MAT + c, 1)] = jnp.where(first, roll(low, 4, 0), high)[None]
            else:
                sx[1, pl.ds(g * MAT + c, 1)] = jnp.where(first, low, roll(high, 4, 0))[None]
    for c in range(2 * MAT):
        lk[pl.ds(g * 2 * MAT + c, 1)] = links_ref[c][None]

    spack = [source_ref[c] for c in range(COMPS)]

    def corner_tiles(tiles, par):
        for k, row in enumerate((7, 4, 3, 0)):
            tile = jnp.zeros((8, lanes), jnp.float32)
            for c in range(COMPS):
                tile = jnp.where(sub == c, jnp.broadcast_to(tiles[c][row:row + 1], (8, lanes)), tile)
            cs[par, k] = tile

    corner_dev = ((g, t_up, x_up), (g, t_dn, x_up), (g, t_up, x_dn), (g, t_dn, x_dn))

    def halo(par):
        routes = ((g, zt, x_up), (g, zt, x_dn), (g, t_up, xy), (g, t_dn, xy))
        found = []
        for k in range(4):
            found.append(copy(cs.at[par, k], cr.at[par, k], hsend.at[par, 4 + k], hrecv.at[par, 4 + k], corner_dev[k]))
        for k in range(4):
            found.append(copy(ws.at[par], wr.at[par, k], hsend.at[par, k], hrecv.at[par, k], routes[k]))
        return found

    def send_part(par):
        def go(p):
            copy(part.at[par, me], part.at[par, me], psend.at[par, p], precv.at[par, me],
                 (g,) + place(lax.rem(me + p, n_all))[1:]).start()
        each(n_all, go)

    def wait_part(par):
        def go(p):
            there = lax.rem(me + n_all - p, n_all)
            done = copy(part.at[par, there], part.at[par, there], psend.at[par, p], precv.at[par, there],
                        (g,) + place(there)[1:])
            done.wait_recv()
            done.wait_send()
        each(n_all, go)

    def dots(rows):
        tile = jnp.zeros((8, lanes), jnp.float32)
        for k, row in enumerate(rows):
            tile = jnp.where(sub == k, jnp.broadcast_to(jnp.sum(row, axis=0, keepdims=True), (8, lanes)), tile)
        tile = tile + roll(tile, 2 * quarter, 1)
        tile = tile + roll(tile, quarter, 1)
        return jnp.sum(jnp.where(home, tile, 0.0), axis=0, keepdims=True)

    def summed(par):
        if n_all <= 32:
            level = [part[par, j] for j in range(n_all)]
            while len(level) > 1:
                odd = level[len(level) // 2 * 2:]
                level = [level[k] + level[k + 1] for k in range(0, len(level) - 1, 2)] + odd
            total = level[0]
        else:
            total = lax.fori_loop(1, n_all, lambda j, acc: acc + part[par, j], part[par, 0])
        split = jnp.where(home, jnp.broadcast_to(total, (8, lanes)), 0.0)
        return jnp.broadcast_to(jnp.sum(split, axis=1, keepdims=True), (8, lanes))

    def fill(values, k):
        return jnp.broadcast_to(values[k:k + 1], (16, lanes))

    def inner(left, right):
        total = left[0] * right[0]
        for c in range(1, COMPS):
            total = total + left[c] * right[c]
        return total

    corner_tiles(spack, 0)
    for c in range(COMPS):
        ws[0, c] = spack[c]
    part[0, pl.ds(me, 1)] = dots([inner(spack, spack)])[None]

    pl.semaphore_wait(barrier, n_grp * n_all - 1)

    half = 2 * MAT
    to_pair = copy(links_ref, lk.at[pl.ds(g * half, half)], lsend.at[0], lrecv.at[0], (other, zt, xy))
    to_pair.start()

    def link_faces(h, src, slot):
        return [
            copy(sx.at[0, pl.ds(h * MAT, MAT)], xfar.at[0, pl.ds(h * MAT, MAT)], lsend.at[slot], lrecv.at[slot], (g, zt, x_up)),
            copy(sx.at[1, pl.ds(h * MAT, MAT)], xfar.at[1, pl.ds(h * MAT, MAT)], lsend.at[slot + 1], lrecv.at[slot + 1], (g, zt, x_dn)),
            copy(src, tfar.at[0, pl.ds(h * half, half)], lsend.at[slot + 2], lrecv.at[slot + 2], (g, t_up, xy)),
            copy(src, tfar.at[1, pl.ds(h * half, half)], lsend.at[slot + 3], lrecv.at[slot + 3], (g, t_dn, xy)),
        ]

    near = link_faces(g, links_ref, 1)
    for item in near:
        item.start()
    send_part(0)
    for item in halo(0):
        item.start()

    to_pair.wait_recv()
    for c in range(MAT):
        low, high = lk[other * half + c], lk[other * half + MAT + c]
        sx[0, pl.ds(other * MAT + c, 1)] = jnp.where(first, roll(low, 4, 0), high)[None]
        sx[1, pl.ds(other * MAT + c, 1)] = jnp.where(first, low, roll(high, 4, 0))[None]
    for c in range(PAIRS):
        sx2[c] = jnp.where(first, lk[c], roll(lk[PAIRS + c], 4, 0))
    for c in range(MAT):
        cs_ll[c:c + 1] = lk[c][7:8]
        cs_ll[MAT + c:MAT + c + 1] = lk[3 * MAT + c][7:8]
        cs_hl[c:c + 1] = lk[3 * MAT + c][3:4]
        cs_lh[c:c + 1] = lk[c][4:5]
    far = link_faces(other, lk.at[pl.ds(other * half, half)], 5) + [
        copy(sx2, xtwo, lsend.at[9], lrecv.at[9], (g, zt, x_up)),
        copy(cs_ll, c_ll, lsend.at[10], lrecv.at[10], corner_dev[0]),
        copy(cs_hl, c_hl, lsend.at[11], lrecv.at[11], corner_dev[2]),
        copy(cs_lh, c_lh, lsend.at[12], lrecv.at[12], corner_dev[1]),
    ]
    for item in far:
        item.start()

    def pick(ref, c):
        return jnp.broadcast_to(ref[c:c + 1], (8, lanes))

    def widen(c, x, mine, low, high):
        between = jnp.where(late, low, high)
        return jnp.where(own, roll(mine, 2 - 4 * x, 0), roll(between, 6 - 4 * x, 0))

    def far_rows(block, low_corner, high_corner, x):
        row = jnp.where(own, roll(block, 2 - 4 * x, 0), 0.0)
        if low_corner is not None:
            row = jnp.where(sub == 1, low_corner, row)
        if high_corner is not None:
            row = jnp.where(sub == 6, high_corner, row)
        return row

    def extend(par, c):
        mine = ws[par, c]
        corner = [jnp.broadcast_to(cr[par, k, c:c + 1], (8, lanes)) for k in range(4)]
        return [
            far_rows(wr[par, 0, c], None, None, 0),
            far_rows(wr[par, 0, c], corner[0], corner[1], 1),
            widen(c, 0, mine, wr[par, 2, c], wr[par, 3, c]),
            widen(c, 1, mine, wr[par, 2, c], wr[par, 3, c]),
            far_rows(wr[par, 1, c], corner[2], corner[3], 0),
            far_rows(wr[par, 1, c], None, None, 1),
        ]

    rows16 = lax.broadcasted_iota(jnp.int32, (16, lanes), 0)
    shift_rows = jnp.zeros((16, lanes), jnp.float32)
    residue_rows = jnp.zeros((16, lanes), jnp.float32)
    for k in range(nshift):
        shift_rows = jnp.where(rows16 == k, shifts_ref[k], shift_rows)
        residue_rows = jnp.where(rows16 == k, residues_ref[k], residue_rows)
    mass_sq = mass_ref[0] * mass_ref[0]

    for c in range(COMPS):
        rpack[c] = spack[c]
        out_ref[c] = jnp.zeros((8, lanes), jnp.float32)
        for k in range(nshift):
            shiftdirs[k, c] = spack[c]

    for item in near[2:] + far[2:4]:
        item.wait()
    to_pair.wait_send()

    t_at = lax.rem(zt * cells_t + sub - 2 + n_zt * cells_t, n_zt * cells_t)
    edge = jnp.where(t_at == n_zt * cells_t - 1, -0.5, 0.5)
    yz_sign = (1 - 2 * lax.rem(ycoord + zcoord, 2)).astype(jnp.float32)
    y_sign = (1 - 2 * lax.rem(ycoord, 2)).astype(jnp.float32)

    def z_up(v):
        cond = jnp.broadcast_to(zcoord == NZ - 1, v.shape)
        return jnp.where(cond, roll(v, NZ - 1, v.ndim - 1), roll(v, -1, v.ndim - 1))

    def z_dn(v):
        cond = jnp.broadcast_to(zcoord == 0, v.shape)
        return jnp.where(cond, roll(v, 1 - NZ, v.ndim - 1), roll(v, 1, v.ndim - 1))

    def wide_link(d, c, e):
        at = d * MAT + c
        sign = -1.0 if e % 2 else 1.0
        if e in (2, 3):
            value = widen(c, e - 2, lk[at], tfar[0, at], tfar[1, at])
        elif e == 0:
            value = far_rows(xtwo[c % PAIRS], None, None, c // PAIRS)
        elif e == 1:
            low = pick(c_ll, c) if d == 0 else (pick(c_ll, MAT + c) if d == 3 else None)
            value = far_rows(xfar[0, (d // 2) * MAT + c], low, pick(c_lh, c) if d == 0 else None, d % 2)
        else:
            value = far_rows(xfar[1, (d // 2) * MAT + c], pick(c_hl, c) if d == 3 else None, None, d % 2)
        if d == 0:
            return 0.5 * value
        if d == 1:
            return (0.5 * sign) * value
        if d == 2:
            return (0.5 * sign) * y_sign * value
        return sign * yz_sign * edge * value

    def build(rows):
        for part_no in range(2):
            for i in range(3):
                for j in range(3):
                    c = part_no * PAIRS + i * 3 + j
                    flip = part_no * PAIRS + j * 3 + i
                    back = 1.0 if part_no else -1.0
                    for e in rows:
                        wx = wide_link(0, c, e)
                        if e > 0:
                            gauge[0, c, e - 1] = wx
                        if e < 4:
                            gauge[1, flip, e] = back * wx
                        if e == 0:
                            continue
                        wz = wide_link(2, c, e)
                        gauge[3, c, e - 1] = wz
                        gauge[4, flip, e - 1] = back * z_dn(wz)
                        wt = wide_link(3, c, e)
                        gauge[5, c, e - 1] = wt
                        gauge[6, flip, e - 1] = back * roll(wt, 1, 0)
                        wy = wide_link(1, c, e)
                        turned = wide_link(1, flip, e)
                        gauge[2, c, e - 1] = wy + back * roll(turned, NZ, 1)

    build((2, 3))
    for item in near[:2] + far[:2] + far[4:]:
        item.wait()
    build((0, 1, 4))

    def finish_halo(par):
        for item in halo(par):
            item.wait()

    wait_part(0)
    finish_halo(0)
    for c in range(COMPS):
        wide = extend(0, c)
        for e in range(6):
            dirn[c, e] = wide[e]
            resid[c, e] = wide[e]
    norm = fill(summed(0), 0)

    def hop(field, e0):
        total = [None] * COMPS
        terms = (
            (0, lambda c: field[c, e0 + 1:e0 + 3]),
            (1, lambda c: field[c, e0 - 1:e0 + 1]),
            (2, lambda c: roll(field[c, e0:e0 + 2], NZ, 2)),
            (3, lambda c: z_up(field[c, e0:e0 + 2])),
            (4, lambda c: z_dn(field[c, e0:e0 + 2])),
            (5, lambda c: roll(field[c, e0:e0 + 2], -1, 1)),
            (6, lambda c: roll(field[c, e0:e0 + 2], 1, 1)),
        )
        for term, shifted in terms:
            v = [shifted(c) for c in range(COMPS)]
            for i in range(3):
                for j in range(3):
                    wre = gauge[term, i * 3 + j, e0 - 1:e0 + 1]
                    wim = gauge[term, PAIRS + i * 3 + j, e0 - 1:e0 + 1]
                    re = wre * v[j] - wim * v[3 + j]
                    im = wre * v[3 + j] + wim * v[j]
                    total[i] = re if total[i] is None else total[i] + re
                    total[3 + i] = im if total[3 + i] is None else total[3 + i] + im
        return total

    def image_of():
        for e0 in (1, 3):
            for c, value in enumerate(hop(dirn, e0)):
                mid[c, e0:e0 + 2] = value
        image = hop(mid, 2)
        packed = []
        dpack = []
        for c in range(COMPS):
            d2, d3 = dirn[c, 2], dirn[c, 3]
            dp = jnp.where(first, roll(d2, -2, 0), roll(d3, 2, 0))
            wp = jnp.where(first, roll(image[c][0], -2, 0), roll(image[c][1], 2, 0))
            dpack.append(dp)
            packed.append(mass_sq * dp - wp)
        return packed, dpack

    def row(values, k):
        return jnp.broadcast_to(values[k:k + 1], (8, lanes))

    def accumulate(gain):
        for c in range(COMPS):
            total = out_ref[c]
            for k in range(nshift):
                total = total + row(gain, k) * shiftdirs[k, c]
            out_ref[c] = total

    def catch_up(gain, zeta_now, beta_shift):
        accumulate(gain)
        for k in range(nshift):
            zk, bk = row(zeta_now, k), row(beta_shift, k)
            for c in range(COMPS):
                shiftdirs[k, c] = zk * rpack[c] + bk * shiftdirs[k, c]

    def iterate(step, last):
        norm, zeta, zeta_old, alpha_old, beta_old, gain, beta_shift, along, score = [state[k] for k in range(9)]
        par = step % 2 if last else lax.rem(step, 2)
        packed, dpack = image_of()
        res = [rpack[c] for c in range(COMPS)]
        part[par, pl.ds(me, 1)] = dots([inner(dpack, packed), inner(res, packed), inner(packed, packed), inner(spack, res)])[None]
        send_part(par)
        if not last:
            corner_tiles(packed, par)
            for c in range(COMPS):
                ws[par, c] = packed[c]
            for item in halo(par):
                item.start()
        catch_up(gain, zeta, beta_shift)
        wait_part(par)
        sums = summed(par)
        alpha = norm / fill(sums, 0)
        zeta_new = zeta * zeta_old * alpha_old / (
            alpha * beta_old * (zeta_old - zeta) + zeta_old * alpha_old * (1.0 + shift_rows * alpha)
        )
        ratio = zeta_new / zeta
        along = zeta * fill(sums, 3) + beta_shift * along
        gain = residue_rows * alpha * ratio
        score = score + gain * along
        if last:
            return gain, score
        norm_next = norm - 2.0 * alpha * fill(sums, 1) + alpha * alpha * fill(sums, 2)
        beta = norm_next / norm
        beta_shift = beta * ratio * ratio
        finish_halo(par)
        step_a, step_b = row(alpha, 0), row(beta, 0)
        for c in range(COMPS):
            rpack[c] = rpack[c] - step_a * ws[par, c]
            wide = extend(par, c)
            for e in range(6):
                fresh = resid[c, e] - step_a * wide[e]
                resid[c, e] = fresh
                dirn[c, e] = fresh + step_b * dirn[c, e]
        for k, value in enumerate((norm_next, zeta_new, zeta, alpha, beta, gain, beta_shift, along, score)):
            state[k] = value

    one = jnp.ones((16, lanes), jnp.float32)
    none = jnp.zeros((16, lanes), jnp.float32)

    def body(step, carry):
        iterate(step, False)
        return carry

    for k, value in enumerate((norm, one, one, one, none, none, none, none, none)):
        state[k] = value
    lax.fori_loop(1, ITERS, body, 0)
    gain, score = iterate(ITERS, True)
    act[g] = jnp.sum(score, axis=0, keepdims=True)

    def swap(p):
        device = (lax.rem(g + p, n_grp), zt, xy)
        return copy(act.at[g], act.at[g], asend.at[p], arecv.at[g], device)

    def swapped(p):
        there = lax.rem(g + n_grp - p, n_grp)
        return copy(act.at[there], act.at[there], asend.at[p], arecv.at[there], (there, zt, xy))

    for p in range(1, n_grp):
        swap(p).start()
    accumulate(gain)
    for p in range(1, n_grp):
        swapped(p).wait_recv()
        swap(p).wait_send()
    total = act[0]
    for k in range(1, n_grp):
        total = total + act[k]
    sites = n_grp * n_all * cells_x * cells_t * lanes
    action_ref[0] = jnp.max(total) * (1.0 / sites)


def on_device(sizes, source, links, shifts, residues, mass):
    n_grp, n_zt, n_xy = sizes
    cells_x, cells_t, lanes = source.shape[3:]
    n_all = n_zt * n_xy
    f32 = jnp.float32
    tiles = lambda *lead: pltpu.VMEM(lead + (8, lanes), f32)
    rows = lambda count: pltpu.VMEM((count, lanes), f32)
    nshift = shifts.shape[0]
    vmem = pl.BlockSpec(memory_space=pltpu.VMEM)
    smem = pl.BlockSpec(memory_space=pltpu.SMEM)
    dma = pltpu.SemaphoreType.DMA
    rational, action = pl.pallas_call(
        functools.partial(kernel, (n_grp, n_zt, n_xy, cells_x, cells_t)),
        out_shape=(
            jax.ShapeDtypeStruct((COMPS, 8, lanes), f32),
            jax.ShapeDtypeStruct((1,), f32),
        ),
        in_specs=[pl.BlockSpec(memory_space=pl.ANY)] * 2 + [smem] * 3,
        out_specs=(vmem, smem),
        scratch_shapes=[
            tiles(4 * MAT), tiles(2, 4 * MAT), tiles(2, 2 * MAT), tiles(PAIRS), tiles(2, 2 * MAT), tiles(PAIRS),
            rows(40), rows(24), rows(24), rows(40), rows(24), rows(24),
            tiles(7, MAT, 4), tiles(COMPS, 6), tiles(COMPS, 6), tiles(COMPS, 6),
            tiles(nshift, COMPS), tiles(COMPS), tiles(2, COMPS), tiles(2, 4, COMPS),
            tiles(2, 4), tiles(2, 4), pltpu.VMEM((2, n_all, 1, lanes), f32), pltpu.VMEM((n_grp, 1, lanes), f32),
            pltpu.VMEM((9, 16, lanes), f32), tiles(COMPS), tiles(2 * MAT), dma((2,)),
            dma((13,)), dma((13,)), dma((2, 8)), dma((2, 8)),
            dma((2, n_all)), dma((2, n_all)), dma((n_grp,)), dma((n_grp,)),
        ],
        compiler_params=pltpu.CompilerParams(collective_id=0, has_side_effects=True),
    )(
        source.reshape(COMPS, 8, lanes), links.reshape(2 * MAT, 8, lanes), shifts, residues, mass
    )
    return rational.reshape(source.shape), action


def solution(mesh):
    sizes = tuple(mesh.shape[name] for name in ("grp", "zt", "xy"))
    field = P("grp", None, None, "xy", "zt", None)
    return jax.shard_map(
        functools.partial(on_device, sizes),
        mesh=mesh,
        in_specs=(field, P("grp", None, None, None, "xy", "zt", None), P(), P(), P()),
        out_specs=(field, P()),
        check_vma=False,
    )
```

profile of v0, /device:TPU:0, one launch (start us, length us, event | category | flops | bytes accessed | tf_op | source)
XLA Modules:
  0.0 67.7 jit_solution(3910357228975687501)
XLA Ops:
  1.3 63.3 %shard_map.68 = (f32[6,8,128]{2,1,0:T(8,128)}, f32[1]{0:T(128)}) custom-call(f32[6,8,128]{2,1,0:T(8,128)} %bitcast.5, f32[36,8,128]{2,1,0:T(8,128)} %bitcast.3, f32[12]{0:T(128)} %shifts_ref.1, f32[12]{0:T(128)} %residues_ref.1, f32[1]{0:T(128)S(6)} %copy.9.mass_ref), custom_call_target="tpu_custom_call" | custom-call | tf_op jit(solution)/shard_map/pallas_call | solution.py:471
  64.5 1.3 %copy.10 = f32[1,2,3,2,4,128]{5,4,3,2,1,0:T(4,128)} copy(f32[1,2,3,2,4,128]{5,4,3,2,1,0:T(4,128)} %bitcast.4) | data formatting | bytes 49152
where the time goes:
time: 67.9 us; the launch traced here: 67.7 us
  Pallas kernels  63.3 us (93%)
  between operations  3.05 us (4%)
  local copies, waits for them, and re-layouts  1.35 us (2%)
    pallas_call x1, Pallas kernels, on_device(): pl.pallas_call(functools.partial(kernel, (n_grp, n_zt, n_xy, cells_x, cel...  63.3 us

commit v1 on v0

--- a/solution.py
+++ b/solution.py
@@ -21,10 +21,11 @@
 
 
 def kernel(
-    dims, source_hbm, links_hbm, shifts_ref, residues_ref, mass_ref, out_ref, action_ref,
-    lk, tfar, xfar, xtwo, sx, sx2, cs_ll, cs_hl, cs_lh, c_ll, c_hl, c_lh,
-    gauge, dirn, resid, mid, shiftdirs, rpack, ws, wr, cs, cr, part, act,
-    state, source_ref, links_ref, isem, lsend, lrecv, hsend, hrecv, psend, precv, asend, arecv,
+    dims, source_hbm, links_hbm, shifts_hbm, residues_hbm, mass_hbm, out_ref, action_ref,
+    lk, tfar, xfar, xtwo, sx, st, sx2, cs_ll, cs_hl, cs_lh, c_ll, c_hl, c_lh,
+    gauge, dirn, resid, mid, shiftdirs, rpack, ws, cs, hb, part, cross,
+    state, mine, theirs, source_ref, links_ref, shifts_ref, residues_ref, mass_ref,
+    isem, lsend, lrecv, hsend, hrecv, psend, precv, asend, arecv,
 ):
     n_grp, n_zt, n_xy, cells_x, cells_t = dims
     lanes = NY * NZ
@@ -69,9 +70,15 @@
 
     fetch_links = pltpu.make_async_copy(links_hbm, links_ref, isem.at[0])
     fetch_source = pltpu.make_async_copy(source_hbm, source_ref, isem.at[1])
+    each(n_grp * n_all, greet)
     fetch_links.start()
     fetch_source.start()
-    each(n_grp * n_all, greet)
+    scalars = [
+        pltpu.make_async_copy(src, dst, isem.at[2 + k])
+        for k, (src, dst) in enumerate(((shifts_hbm, shifts_ref), (residues_hbm, residues_ref), (mass_hbm, mass_ref)))
+    ]
+    for item in scalars:
+        item.start()
     fetch_links.wait()
     fetch_source.wait()
 
@@ -85,6 +92,10 @@
     first = sub < cells_t
     late = lax.rem(sub, cells_t) >= 2
 
+    def t_faces(c, one, two):
+        st[0, pl.ds(c, 1)] = jnp.where(late, one, roll(two, -2, 0))[None]
+        st[1, pl.ds(c, 1)] = jnp.where(late, roll(two, 2, 0), one)[None]
+
     for d in range(2):
         for c in range(MAT):
             low, high = links_ref[c], links_ref[MAT + c]
@@ -92,6 +103,8 @@
                 sx[0, pl.ds(g * MAT + c, 1)] = jnp.where(first, roll(low, 4, 0), high)[None]
             else:
                 sx[1, pl.ds(g * MAT + c, 1)] = jnp.where(first, low, roll(high, 4, 0))[None]
+    for c in range(MAT):
+        t_faces(g * MAT + c, links_ref[c], links_ref[MAT + c])
     for c in range(2 * MAT):
         lk[pl.ds(g * 2 * MAT + c, 1)] = links_ref[c][None]
 
@@ -110,24 +123,26 @@
         routes = ((g, zt, x_up), (g, zt, x_dn), (g, t_up, xy), (g, t_dn, xy))
         found = []
         for k in range(4):
-            found.append(copy(cs.at[par, k], cr.at[par, k], hsend.at[par, 4 + k], hrecv.at[par, 4 + k], corner_dev[k]))
+            found.append(copy(cs.at[par, pl.ds(k, 1)], hb.at[par, pl.ds(4 * COMPS + k, 1)], hsend.at[par], hrecv.at[par], corner_dev[k]))
         for k in range(4):
-            found.append(copy(ws.at[par], wr.at[par, k], hsend.at[par, k], hrecv.at[par, k], routes[k]))
+            found.append(copy(ws.at[par], hb.at[par, pl.ds(k * COMPS, COMPS)], hsend.at[par], hrecv.at[par], routes[k]))
         return found
 
     def send_part(par):
         def go(p):
-            copy(part.at[par, me], part.at[par, me], psend.at[par, p], precv.at[par, me],
+            copy(part.at[par, me], part.at[par, me], psend.at[par], precv.at[par],
                  (g,) + place(lax.rem(me + p, n_all))[1:]).start()
         each(n_all, go)
 
     def wait_part(par):
+        rest = part.at[par, pl.ds(0, n_all - 1)]
+        copy(rest, rest, psend.at[par], precv.at[par], corner_dev[0]).wait()
+
+    def send_cross(par):
         def go(p):
-            there = lax.rem(me + n_all - p, n_all)
-            done = copy(part.at[par, there], part.at[par, there], psend.at[par, p], precv.at[par, there],
-                        (g,) + place(there)[1:])
-            done.wait_recv()
-            done.wait_send()
+            copy(part.at[par, me], cross.at[me], asend.at[0], arecv.at[0],
+                 (other,) + place(lax.rem(me + p, n_all))[1:]).start()
+        go(0)
         each(n_all, go)
 
     def dots(rows):
@@ -138,15 +153,15 @@
         tile = tile + roll(tile, quarter, 1)
         return jnp.sum(jnp.where(home, tile, 0.0), axis=0, keepdims=True)
 
-    def summed(par):
+    def summed(row_of):
         if n_all <= 32:
-            level = [part[par, j] for j in range(n_all)]
+            level = [row_of(j) for j in range(n_all)]
             while len(level) > 1:
                 odd = level[len(level) // 2 * 2:]
                 level = [level[k] + level[k + 1] for k in range(0, len(level) - 1, 2)] + odd
             total = level[0]
         else:
-            total = lax.fori_loop(1, n_all, lambda j, acc: acc + part[par, j], part[par, 0])
+            total = lax.fori_loop(1, n_all, lambda j, acc: acc + row_of(j), row_of(0))
         split = jnp.where(home, jnp.broadcast_to(total, (8, lanes)), 0.0)
         return jnp.broadcast_to(jnp.sum(split, axis=1, keepdims=True), (8, lanes))
 
@@ -170,16 +185,16 @@
     to_pair = copy(links_ref, lk.at[pl.ds(g * half, half)], lsend.at[0], lrecv.at[0], (other, zt, xy))
     to_pair.start()
 
-    def link_faces(h, src, slot):
+    def link_faces(h):
+        span = pl.ds(h * MAT, MAT)
         return [
-            copy(sx.at[0, pl.ds(h * MAT, MAT)], xfar.at[0, pl.ds(h * MAT, MAT)], lsend.at[slot], lrecv.at[slot], (g, zt, x_up)),
-            copy(sx.at[1, pl.ds(h * MAT, MAT)], xfar.at[1, pl.ds(h * MAT, MAT)], lsend.at[slot + 1], lrecv.at[slot + 1], (g, zt, x_dn)),
-            copy(src, tfar.at[0, pl.ds(h * half, half)], lsend.at[slot + 2], lrecv.at[slot + 2], (g, t_up, xy)),
-            copy(src, tfar.at[1, pl.ds(h * half, half)], lsend.at[slot + 3], lrecv.at[slot + 3], (g, t_dn, xy)),
+            copy(sx.at[0, span], xfar.at[0, span], lsend.at[1], lrecv.at[1], (g, zt, x_up)),
+            copy(sx.at[1, span], xfar.at[1, span], lsend.at[1], lrecv.at[1], (g, zt, x_dn)),
+            copy(st.at[0, span], tfar.at[0, span], lsend.at[2], lrecv.at[2], (g, t_up, xy)),
+            copy(st.at[1, span], tfar.at[1, span], lsend.at[2], lrecv.at[2], (g, t_dn, xy)),
         ]
 
-    near = link_faces(g, links_ref, 1)
-    for item in near:
+    for item in link_faces(g):
         item.start()
     send_part(0)
     for item in halo(0):
@@ -190,6 +205,7 @@
         low, high = lk[other * half + c], lk[other * half + MAT + c]
         sx[0, pl.ds(other * MAT + c, 1)] = jnp.where(first, roll(low, 4, 0), high)[None]
         sx[1, pl.ds(other * MAT + c, 1)] = jnp.where(first, low, roll(high, 4, 0))[None]
+        t_faces(other * MAT + c, low, high)
     for c in range(PAIRS):
         sx2[c] = jnp.where(first, lk[c], roll(lk[PAIRS + c], 4, 0))
     for c in range(MAT):
@@ -197,13 +213,13 @@
         cs_ll[MAT + c:MAT + c + 1] = lk[3 * MAT + c][7:8]
         cs_hl[c:c + 1] = lk[3 * MAT + c][3:4]
         cs_lh[c:c + 1] = lk[c][4:5]
-    far = link_faces(other, lk.at[pl.ds(other * half, half)], 5) + [
-        copy(sx2, xtwo, lsend.at[9], lrecv.at[9], (g, zt, x_up)),
-        copy(cs_ll, c_ll, lsend.at[10], lrecv.at[10], corner_dev[0]),
-        copy(cs_hl, c_hl, lsend.at[11], lrecv.at[11], corner_dev[2]),
-        copy(cs_lh, c_lh, lsend.at[12], lrecv.at[12], corner_dev[1]),
+    rest = [
+        copy(sx2, xtwo, lsend.at[3], lrecv.at[3], (g, zt, x_up)),
+        copy(cs_ll, c_ll, lsend.at[4], lrecv.at[4], corner_dev[0]),
+        copy(cs_hl, c_hl, lsend.at[5], lrecv.at[5], corner_dev[2]),
+        copy(cs_lh, c_lh, lsend.at[6], lrecv.at[6], corner_dev[1]),
     ]
-    for item in far:
+    for item in rest + link_faces(other):
         item.start()
 
     def pick(ref, c):
@@ -222,17 +238,20 @@
         return row
 
     def extend(par, c):
-        mine = ws[par, c]
-        corner = [jnp.broadcast_to(cr[par, k, c:c + 1], (8, lanes)) for k in range(4)]
+        own_part = ws[par, c]
+        corner = [jnp.broadcast_to(hb[par, 4 * COMPS + k, c:c + 1], (8, lanes)) for k in range(4)]
+        x_lo, x_hi, t_lo, t_hi = [hb[par, k * COMPS + c] for k in range(4)]
         return [
-            far_rows(wr[par, 0, c], None, None, 0),
-            far_rows(wr[par, 0, c], corner[0], corner[1], 1),
-            widen(c, 0, mine, wr[par, 2, c], wr[par, 3, c]),
-            widen(c, 1, mine, wr[par, 2, c], wr[par, 3, c]),
-            far_rows(wr[par, 1, c], corner[2], corner[3], 0),
-            far_rows(wr[par, 1, c], None, None, 1),
+            far_rows(x_lo, None, None, 0),
+            far_rows(x_lo, corner[0], corner[1], 1),
+            widen(c, 0, own_part, t_lo, t_hi),
+            widen(c, 1, own_part, t_lo, t_hi),
+            far_rows(x_hi, corner[2], corner[3], 0),
+            far_rows(x_hi, None, None, 1),
         ]
 
+    for item in scalars:
+        item.wait()
     rows16 = lax.broadcasted_iota(jnp.int32, (16, lanes), 0)
     shift_rows = jnp.zeros((16, lanes), jnp.float32)
     residue_rows = jnp.zeros((16, lanes), jnp.float32)
@@ -247,8 +266,7 @@
         for k in range(nshift):
             shiftdirs[k, c] = spack[c]
 
-    for item in near[2:] + far[2:4]:
-        item.wait()
+    copy(st, tfar, lsend.at[2], lrecv.at[2], (g, t_up, xy)).wait()
     to_pair.wait_send()
 
     t_at = lax.rem(zt * cells_t + sub - 2 + n_zt * cells_t, n_zt * cells_t)
@@ -268,7 +286,10 @@
         at = d * MAT + c
         sign = -1.0 if e % 2 else 1.0
         if e in (2, 3):
-            value = widen(c, e - 2, lk[at], tfar[0, at], tfar[1, at])
+            low, high = tfar[0, (d // 2) * MAT + c], tfar[1, (d // 2) * MAT + c]
+            if d % 2:
+                low, high = roll(low, 2, 0), roll(high, -2, 0)
+            value = widen(c, e - 2, lk[at], low, high)
         elif e == 0:
             value = far_rows(xtwo[c % PAIRS], None, None, c // PAIRS)
         elif e == 1:
@@ -310,13 +331,12 @@
                         gauge[2, c, e - 1] = wy + back * roll(turned, NZ, 1)
 
     build((2, 3))
-    for item in near[:2] + far[:2] + far[4:]:
+    for item in [copy(sx, xfar, lsend.at[1], lrecv.at[1], (g, zt, x_up))] + rest:
         item.wait()
     build((0, 1, 4))
 
     def finish_halo(par):
-        for item in halo(par):
-            item.wait()
+        copy(hb.at[par], hb.at[par], hsend.at[par], hrecv.at[par], corner_dev[0]).wait()
 
     wait_part(0)
     finish_halo(0)
@@ -325,7 +345,7 @@
         for e in range(6):
             dirn[c, e] = wide[e]
             resid[c, e] = wide[e]
-    norm = fill(summed(0), 0)
+    norm = fill(summed(lambda j: part[0, j]), 0)
 
     def hop(field, e0):
         total = [None] * COMPS
@@ -382,14 +402,34 @@
             for c in range(COMPS):
                 shiftdirs[k, c] = zk * rpack[c] + bk * shiftdirs[k, c]
 
+    lane16 = lax.broadcasted_iota(jnp.int32, (16, lanes), 1)
+    swap = copy(mine, theirs, asend.at[1], arecv.at[1], (other, zt, xy))
+
+    def closing(sums, values):
+        norm, zeta, zeta_old, alpha_old, beta_old, beta_shift, along, score = values
+        alpha = norm / fill(sums, 0)
+        zeta_new = zeta * zeta_old * alpha_old / (
+            alpha * beta_old * (zeta_old - zeta) + zeta_old * alpha_old * (1.0 + shift_rows * alpha)
+        )
+        gain = residue_rows * alpha * (zeta_new / zeta)
+        return gain, score + gain * (zeta * fill(sums, 3) + beta_shift * along)
+
     def iterate(step, last):
-        norm, zeta, zeta_old, alpha_old, beta_old, gain, beta_shift, along, score = [state[k] for k in range(9)]
+        norm, zeta, zeta_old, alpha_old, beta_old, beta_shift, along, score, gain = [state[k] for k in range(9)]
         par = step % 2 if last else lax.rem(step, 2)
+        if last:
+            packed_state = norm
+            for k in range(1, 8):
+                packed_state = jnp.where(lane16 == k, state[k], packed_state)
+            mine[...] = packed_state
+            swap.start()
         packed, dpack = image_of()
         res = [rpack[c] for c in range(COMPS)]
         part[par, pl.ds(me, 1)] = dots([inner(dpack, packed), inner(res, packed), inner(packed, packed), inner(spack, res)])[None]
         send_part(par)
-        if not last:
+        if last:
+            send_cross(par)
+        else:
             corner_tiles(packed, par)
             for c in range(COMPS):
                 ws[par, c] = packed[c]
@@ -397,7 +437,11 @@
                 item.start()
         catch_up(gain, zeta, beta_shift)
         wait_part(par)
-        sums = summed(par)
+        sums = summed(lambda j: part[par, j])
+        if last:
+            gain, score = closing(sums, [state[k] for k in range(8)])
+            accumulate(gain)
+            return score
         alpha = norm / fill(sums, 0)
         zeta_new = zeta * zeta_old * alpha_old / (
             alpha * beta_old * (zeta_old - zeta) + zeta_old * alpha_old * (1.0 + shift_rows * alpha)
@@ -406,8 +450,6 @@
         along = zeta * fill(sums, 3) + beta_shift * along
         gain = residue_rows * alpha * ratio
         score = score + gain * along
-        if last:
-            return gain, score
         norm_next = norm - 2.0 * alpha * fill(sums, 1) + alpha * alpha * fill(sums, 2)
         beta = norm_next / norm
         beta_shift = beta * ratio * ratio
@@ -420,7 +462,7 @@
                 fresh = resid[c, e] - step_a * wide[e]
                 resid[c, e] = fresh
                 dirn[c, e] = fresh + step_b * dirn[c, e]
-        for k, value in enumerate((norm_next, zeta_new, zeta, alpha, beta, gain, beta_shift, along, score)):
+        for k, value in enumerate((norm_next, zeta_new, zeta, alpha, beta, beta_shift, along, score, gain)):
             state[k] = value
 
     one = jnp.ones((16, lanes), jnp.float32)
@@ -433,28 +475,14 @@
     for k, value in enumerate((norm, one, one, one, none, none, none, none, none)):
         state[k] = value
     lax.fori_loop(1, ITERS, body, 0)
-    gain, score = iterate(ITERS, True)
-    act[g] = jnp.sum(score, axis=0, keepdims=True)
-
-    def swap(p):
-        device = (lax.rem(g + p, n_grp), zt, xy)
-        return copy(act.at[g], act.at[g], asend.at[p], arecv.at[g], device)
-
-    def swapped(p):
-        there = lax.rem(g + n_grp - p, n_grp)
-        return copy(act.at[there], act.at[there], asend.at[p], arecv.at[there], (there, zt, xy))
-
-    for p in range(1, n_grp):
-        swap(p).start()
-    accumulate(gain)
-    for p in range(1, n_grp):
-        swapped(p).wait_recv()
-        swap(p).wait_send()
-    total = act[0]
-    for k in range(1, n_grp):
-        total = total + act[k]
+    score = iterate(ITERS, True)
+    swap.wait()
+    copy(cross, cross, asend.at[0], arecv.at[0], corner_dev[0]).wait()
+    far_state = theirs[...]
+    values = [jnp.broadcast_to(far_state[:, k:k + 1], (16, lanes)) for k in range(8)]
+    total = score + closing(summed(lambda j: cross[j]), values)[1]
     sites = n_grp * n_all * cells_x * cells_t * lanes
-    action_ref[0] = jnp.max(total) * (1.0 / sites)
+    action_ref[0] = jnp.max(jnp.sum(total, axis=0, keepdims=True)) * (1.0 / sites)
 
 
 def on_device(sizes, source, links, shifts, residues, mass):
@@ -471,20 +499,20 @@
     rational, action = pl.pallas_call(
         functools.partial(kernel, (n_grp, n_zt, n_xy, cells_x, cells_t)),
         out_shape=(
-            jax.ShapeDtypeStruct((COMPS, 8, lanes), f32),
-            jax.ShapeDtypeStruct((1,), f32),
+            pltpu.VMEM((COMPS, 8, lanes), f32),
+            pltpu.SMEM((1,), f32),
         ),
-        in_specs=[pl.BlockSpec(memory_space=pl.ANY)] * 2 + [smem] * 3,
+        in_specs=[pl.BlockSpec(memory_space=pltpu.HBM)] * 5,
         out_specs=(vmem, smem),
         scratch_shapes=[
-            tiles(4 * MAT), tiles(2, 4 * MAT), tiles(2, 2 * MAT), tiles(PAIRS), tiles(2, 2 * MAT), tiles(PAIRS),
+            tiles(4 * MAT), tiles(2, 2 * MAT), tiles(2, 2 * MAT), tiles(PAIRS), tiles(2, 2 * MAT), tiles(2, 2 * MAT), tiles(PAIRS),
             rows(40), rows(24), rows(24), rows(40), rows(24), rows(24),
             tiles(7, MAT, 4), tiles(COMPS, 6), tiles(COMPS, 6), tiles(COMPS, 6),
-            tiles(nshift, COMPS), tiles(COMPS), tiles(2, COMPS), tiles(2, 4, COMPS),
-            tiles(2, 4), tiles(2, 4), pltpu.VMEM((2, n_all, 1, lanes), f32), pltpu.VMEM((n_grp, 1, lanes), f32),
-            pltpu.VMEM((9, 16, lanes), f32), tiles(COMPS), tiles(2 * MAT), dma((2,)),
-            dma((13,)), dma((13,)), dma((2, 8)), dma((2, 8)),
-            dma((2, n_all)), dma((2, n_all)), dma((n_grp,)), dma((n_grp,)),
+            tiles(nshift, COMPS), tiles(COMPS), tiles(2, COMPS), tiles(2, 4), tiles(2, 4 * COMPS + 4),
+            pltpu.VMEM((2, n_all, 1, lanes), f32), pltpu.VMEM((n_all, 1, lanes), f32),
+            pltpu.VMEM((9, 16, lanes), f32), rows(16), rows(16), tiles(COMPS), tiles(2 * MAT),
+            pltpu.SMEM((nshift,), f32), pltpu.SMEM((nshift,), f32), pltpu.SMEM((1,), f32), dma((5,)),
+            dma((7,)), dma((7,)), dma((2,)), dma((2,)), dma((2,)), dma((2,)), dma((2,)), dma((2,)),
         ],
         compiler_params=pltpu.CompilerParams(collective_id=0, has_side_effects=True),
     )(

time: 67.9 us -> 61.4 us (0.904)
  Pallas kernels: 63.3 us -> 58.8 us
  between operations: 3.05 us -> 1.8 us
  local copies, waits for them, and re-layouts: 1.35 us -> 0.61 us
    pallas_call x1, Pallas kernels: 63.3 us -> 58.8 us  [on_device(): pl.pallas_call(functools.partial(kernel, (n_grp, n_zt, n_xy, cells_x, cel...]
    unnamed x1, local copies, waits for them, and re-layouts: 1.35 us -> 0.61 us
where the time goes in v1:
time: 61.4 us; the launch traced here: 61.2 us
  Pallas kernels  58.8 us (96%)
  between operations  1.8 us (3%)
    pallas_call x1, Pallas kernels, on_device(): pl.pallas_call(functools.partial(kernel, (n_grp, n_zt, n_xy, cells_x, cel...  58.8 us

profile of v1, /device:TPU:0, one launch (start us, length us, event | category | flops | bytes accessed | tf_op | source)
XLA Modules:
  0.0 61.2 jit_solution(17820442142037293610)
XLA Ops:
  1.3 58.8 %shard_map.68 = (f32[6,8,128]{2,1,0:T(8,128)S(1)}, f32[1]{0:T(128)S(4)}) custom-call(f32[6,8,128]{2,1,0:T(8,128)} %bitcast.5, f32[36,8,128]{2,1,0:T(8,128)} %bitcast.4, f32[12]{0:T(128)} %shifts_hbm.1, f32[12]{0:T(128)} %residues_hbm.1, f32[1]{0:T(128)S(6)} %copy.11.mass_hbm), custom_call_target="tpu_custom_call" | custom-call | tf_op jit(solution)/shard_map/pallas_call | solution.py:499
  60.6 0.6 copy.9

commit v2 on v1

--- a/solution.py
+++ b/solution.py
@@ -23,7 +23,7 @@
 def kernel(
     dims, source_hbm, links_hbm, shifts_hbm, residues_hbm, mass_hbm, out_ref, action_ref,
     lk, tfar, xfar, xtwo, sx, st, sx2, cs_ll, cs_hl, cs_lh, c_ll, c_hl, c_lh,
-    gauge, dirn, resid, mid, shiftdirs, rpack, ws, cs, hb, part, cross,
+    gauge, wide, hop_w, hop_r, mid, dpack_ref, shiftdirs, rpack, ws, cs, hb, part, cross,
     state, mine, theirs, source_ref, links_ref, shifts_ref, residues_ref, mass_ref,
     isem, lsend, lrecv, hsend, hrecv, psend, precv, asend, arecv,
 ):
@@ -62,15 +62,20 @@
 
     barrier = pltpu.get_barrier_semaphore()
 
-    def greet(p):
-        pl.semaphore_signal(
-            barrier, inc=1, device_id=place(lax.rem(me_all + p, n_grp * n_all)),
-            device_id_type=pl.DeviceIdType.MESH,
-        )
+    corner_dev = ((g, t_up, x_up), (g, t_dn, x_up), (g, t_up, x_dn), (g, t_dn, x_dn))
+    partners = ((other, zt, xy), (g, zt, x_up), (g, zt, x_dn), (g, t_up, xy), (g, t_dn, xy)) + corner_dev
+    near_barrier = n_zt <= 4 and n_xy <= 4
+
+    def greet(device):
+        pl.semaphore_signal(barrier, inc=1, device_id=device, device_id_type=pl.DeviceIdType.MESH)
 
     fetch_links = pltpu.make_async_copy(links_hbm, links_ref, isem.at[0])
     fetch_source = pltpu.make_async_copy(source_hbm, source_ref, isem.at[1])
-    each(n_grp * n_all, greet)
+    if near_barrier:
+        for device in partners:
+            greet(device)
+    else:
+        each(n_grp * n_all, lambda p: greet(place(lax.rem(me_all + p, n_grp * n_all))))
     fetch_links.start()
     fetch_source.start()
     scalars = [
@@ -117,15 +122,17 @@
                 tile = jnp.where(sub == c, jnp.broadcast_to(tiles[c][row:row + 1], (8, lanes)), tile)
             cs[par, k] = tile
 
-    corner_dev = ((g, t_up, x_up), (g, t_dn, x_up), (g, t_up, x_dn), (g, t_dn, x_dn))
-
     def halo(par):
-        routes = ((g, zt, x_up), (g, zt, x_dn), (g, t_up, xy), (g, t_dn, xy))
+        k_first = jnp.where(xy == 0, 1, 0)
+        routes = (
+            (k_first, (g, zt, jnp.where(xy == 0, x_dn, x_up))), (1 - k_first, (g, zt, jnp.where(xy == 0, x_up, x_dn))),
+            (2, (g, t_up, xy)), (3, (g, t_dn, xy)),
+        )
         found = []
         for k in range(4):
             found.append(copy(cs.at[par, pl.ds(k, 1)], hb.at[par, pl.ds(4 * COMPS + k, 1)], hsend.at[par], hrecv.at[par], corner_dev[k]))
-        for k in range(4):
-            found.append(copy(ws.at[par], hb.at[par, pl.ds(k * COMPS, COMPS)], hsend.at[par], hrecv.at[par], routes[k]))
+        for k, device in routes:
+            found.append(copy(ws.at[par], hb.at[par, pl.ds(k * COMPS, COMPS)], hsend.at[par], hrecv.at[par], device))
         return found
 
     def send_part(par):
@@ -149,8 +156,7 @@
         tile = jnp.zeros((8, lanes), jnp.float32)
         for k, row in enumerate(rows):
             tile = jnp.where(sub == k, jnp.broadcast_to(jnp.sum(row, axis=0, keepdims=True), (8, lanes)), tile)
-        tile = tile + roll(tile, 2 * quarter, 1)
-        tile = tile + roll(tile, quarter, 1)
+        tile = (tile + roll(tile, 2 * quarter, 1)) + (roll(tile, quarter, 1) + roll(tile, 3 * quarter, 1))
         return jnp.sum(jnp.where(home, tile, 0.0), axis=0, keepdims=True)
 
     def summed(row_of):
@@ -177,9 +183,8 @@
     corner_tiles(spack, 0)
     for c in range(COMPS):
         ws[0, c] = spack[c]
-    part[0, pl.ds(me, 1)] = dots([inner(spack, spack)])[None]
-
-    pl.semaphore_wait(barrier, n_grp * n_all - 1)
+
+    pl.semaphore_wait(barrier, len(partners) if near_barrier else n_grp * n_all - 1)
 
     half = 2 * MAT
     to_pair = copy(links_ref, lk.at[pl.ds(g * half, half)], lsend.at[0], lrecv.at[0], (other, zt, xy))
@@ -196,7 +201,6 @@
 
     for item in link_faces(g):
         item.start()
-    send_part(0)
     for item in halo(0):
         item.start()
 
@@ -338,14 +342,7 @@
     def finish_halo(par):
         copy(hb.at[par], hb.at[par], hsend.at[par], hrecv.at[par], corner_dev[0]).wait()
 
-    wait_part(0)
     finish_halo(0)
-    for c in range(COMPS):
-        wide = extend(0, c)
-        for e in range(6):
-            dirn[c, e] = wide[e]
-            resid[c, e] = wide[e]
-    norm = fill(summed(lambda j: part[0, j]), 0)
 
     def hop(field, e0):
         total = [None] * COMPS
@@ -370,20 +367,27 @@
                     total[3 + i] = im if total[3 + i] is None else total[3 + i] + im
         return total
 
+    def hop_wide(par):
+        for c in range(COMPS):
+            for e, value in enumerate(extend(par, c)):
+                wide[c, e] = value
+        for e0 in (1, 3):
+            for c, value in enumerate(hop(wide, e0)):
+                hop_w[c, e0:e0 + 2] = value
+
+    hop_wide(0)
+    for c in range(COMPS):
+        dpack_ref[c] = spack[c]
+        hop_r[c, 1:5] = hop_w[c, 1:5]
+        mid[c, 1:5] = hop_w[c, 1:5]
+
     def image_of():
-        for e0 in (1, 3):
-            for c, value in enumerate(hop(dirn, e0)):
-                mid[c, e0:e0 + 2] = value
         image = hop(mid, 2)
         packed = []
-        dpack = []
         for c in range(COMPS):
-            d2, d3 = dirn[c, 2], dirn[c, 3]
-            dp = jnp.where(first, roll(d2, -2, 0), roll(d3, 2, 0))
             wp = jnp.where(first, roll(image[c][0], -2, 0), roll(image[c][1], 2, 0))
-            dpack.append(dp)
-            packed.append(mass_sq * dp - wp)
-        return packed, dpack
+            packed.append(mass_sq * dpack_ref[c] - wp)
+        return packed, [dpack_ref[c] for c in range(COMPS)]
 
     def row(values, k):
         return jnp.broadcast_to(values[k:k + 1], (8, lanes))
@@ -436,12 +440,16 @@
             for item in halo(par):
                 item.start()
         catch_up(gain, zeta, beta_shift)
+        if not last:
+            finish_halo(par)
+            hop_wide(par)
         wait_part(par)
         sums = summed(lambda j: part[par, j])
         if last:
             gain, score = closing(sums, [state[k] for k in range(8)])
             accumulate(gain)
             return score
+        norm = jnp.where(step == 1, fill(sums, 3), norm)
         alpha = norm / fill(sums, 0)
         zeta_new = zeta * zeta_old * alpha_old / (
             alpha * beta_old * (zeta_old - zeta) + zeta_old * alpha_old * (1.0 + shift_rows * alpha)
@@ -453,15 +461,15 @@
         norm_next = norm - 2.0 * alpha * fill(sums, 1) + alpha * alpha * fill(sums, 2)
         beta = norm_next / norm
         beta_shift = beta * ratio * ratio
-        finish_halo(par)
         step_a, step_b = row(alpha, 0), row(beta, 0)
         for c in range(COMPS):
-            rpack[c] = rpack[c] - step_a * ws[par, c]
-            wide = extend(par, c)
-            for e in range(6):
-                fresh = resid[c, e] - step_a * wide[e]
-                resid[c, e] = fresh
-                dirn[c, e] = fresh + step_b * dirn[c, e]
+            fresh = rpack[c] - step_a * ws[par, c]
+            rpack[c] = fresh
+            dpack_ref[c] = fresh + step_b * dpack_ref[c]
+            for e in range(1, 5):
+                fresh = hop_r[c, e] - step_a * hop_w[c, e]
+                hop_r[c, e] = fresh
+                mid[c, e] = fresh + step_b * mid[c, e]
         for k, value in enumerate((norm_next, zeta_new, zeta, alpha, beta, beta_shift, along, score, gain)):
             state[k] = value
 
@@ -472,7 +480,7 @@
         iterate(step, False)
         return carry
 
-    for k, value in enumerate((norm, one, one, one, none, none, none, none, none)):
+    for k, value in enumerate((one, one, one, one, none, none, none, none, none)):
         state[k] = value
     lax.fori_loop(1, ITERS, body, 0)
     score = iterate(ITERS, True)
@@ -507,7 +515,7 @@
         scratch_shapes=[
             tiles(4 * MAT), tiles(2, 2 * MAT), tiles(2, 2 * MAT), tiles(PAIRS), tiles(2, 2 * MAT), tiles(2, 2 * MAT), tiles(PAIRS),
             rows(40), rows(24), rows(24), rows(40), rows(24), rows(24),
-            tiles(7, MAT, 4), tiles(COMPS, 6), tiles(COMPS, 6), tiles(COMPS, 6),
+            tiles(7, MAT, 4), tiles(COMPS, 6), tiles(COMPS, 6), tiles(COMPS, 6), tiles(COMPS, 6), tiles(COMPS),
             tiles(nshift, COMPS), tiles(COMPS), tiles(2, COMPS), tiles(2, 4), tiles(2, 4 * COMPS + 4),
             pltpu.VMEM((2, n_all, 1, lanes), f32), pltpu.VMEM((n_all, 1, lanes), f32),
             pltpu.VMEM((9, 16, lanes), f32), rows(16), rows(16), tiles(COMPS), tiles(2 * MAT),

time: 61.4 us -> 60.7 us (0.989)
  Pallas kernels: 58.8 us -> 58.1 us
    pallas_call x1, Pallas kernels: 58.8 us -> 58.1 us  [on_device(): pl.pallas_call(functools.partial(kernel, (n_grp, n_zt, n_xy, cells_x, cel...]
where the time goes in v2:
time: 60.7 us; the launch traced here: 60.6 us
  Pallas kernels  58.1 us (96%)
  between operations  1.8 us (3%)
  local copies, waits for them, and re-layouts  0.61 us (1%)
    pallas_call x1, Pallas kernels, on_device(): pl.pallas_call(functools.partial(kernel, (n_grp, n_zt, n_xy, cells_x, cel...  58.1 us

profile of v2, /device:TPU:0, one launch (start us, length us, event | category | flops | bytes accessed | tf_op | source)
XLA Modules:
  0.0 60.6 jit_solution(15726340248143877530)
XLA Ops:
  1.3 58.1 %shard_map.68 = (f32[6,8,128]{2,1,0:T(8,128)S(1)}, f32[1]{0:T(128)S(4)}) custom-call(f32[6,8,128]{2,1,0:T(8,128)} %bitcast.5, f32[36,8,128]{2,1,0:T(8,128)} %bitcast.4, f32[12]{0:T(128)} %shifts_hbm.1, f32[12]{0:T(128)} %residues_hbm.1, f32[1]{0:T(128)S(6)} %copy.11.mass_hbm), custom_call_target="tpu_custom_call" | custom-call | tf_op jit(solution)/shard_map/pallas_call | solution.py:507
  59.9 0.6 %copy.9 = f32[1,2,3,2,4,128]{5,4,3,2,1,0:T(4,128)} copy(f32[1,2,3,2,4,128]{5,4,3,2,1,0:T(4,128)S(1)} %bitcast.3) | data formatting | bytes 49152

commit v3 on v2

--- a/solution.py
+++ b/solution.py
@@ -25,7 +25,7 @@
     lk, tfar, xfar, xtwo, sx, st, sx2, cs_ll, cs_hl, cs_lh, c_ll, c_hl, c_lh,
     gauge, wide, hop_w, hop_r, mid, dpack_ref, shiftdirs, rpack, ws, cs, hb, part, cross,
     state, mine, theirs, source_ref, links_ref, shifts_ref, residues_ref, mass_ref,
-    isem, lsend, lrecv, hsend, hrecv, psend, precv, asend, arecv,
+    isem, lsend, lrecv, hsend, hrecv, psend, precv, asend, arecv, ready,
 ):
     n_grp, n_zt, n_xy, cells_x, cells_t = dims
     lanes = NY * NZ
@@ -63,8 +63,10 @@
     barrier = pltpu.get_barrier_semaphore()
 
     corner_dev = ((g, t_up, x_up), (g, t_dn, x_up), (g, t_up, x_dn), (g, t_dn, x_dn))
-    partners = ((other, zt, xy), (g, zt, x_up), (g, zt, x_dn), (g, t_up, xy), (g, t_dn, xy)) + corner_dev
+    above = ((g, zt, x_up),) + corner_dev[:2]
+    partners = ((other, zt, xy), (g, t_up, xy), (g, t_dn, xy), (g, zt, x_dn)) + corner_dev[2:]
     near_barrier = n_zt <= 4 and n_xy <= 4
+    at_top, at_bottom = xy == n_xy - 1, xy == 0
 
     def greet(device):
         pl.semaphore_signal(barrier, inc=1, device_id=device, device_id_type=pl.DeviceIdType.MESH)
@@ -74,6 +76,11 @@
     if near_barrier:
         for device in partners:
             greet(device)
+
+        @pl.when(jnp.logical_not(at_top))
+        def _():
+            for device in above:
+                greet(device)
     else:
         each(n_grp * n_all, lambda p: greet(place(lax.rem(me_all + p, n_grp * n_all))))
     fetch_links.start()
@@ -122,18 +129,27 @@
                 tile = jnp.where(sub == c, jnp.broadcast_to(tiles[c][row:row + 1], (8, lanes)), tile)
             cs[par, k] = tile
 
-    def halo(par):
-        k_first = jnp.where(xy == 0, 1, 0)
-        routes = (
-            (k_first, (g, zt, jnp.where(xy == 0, x_dn, x_up))), (1 - k_first, (g, zt, jnp.where(xy == 0, x_up, x_dn))),
-            (2, (g, t_up, xy)), (3, (g, t_dn, xy)),
-        )
-        found = []
+    def face(par, k):
+        device = ((g, zt, x_up), (g, zt, x_dn), (g, t_up, xy), (g, t_dn, xy))[k]
+        return copy(ws.at[par], hb.at[par, pl.ds(k * COMPS, COMPS)], hsend.at[par], hrecv.at[par], device)
+
+    def corner(par, k):
+        return copy(cs.at[par, pl.ds(k, 1)], hb.at[par, pl.ds(4 * COMPS + k, 1)], hsend.at[par], hrecv.at[par], corner_dev[k])
+
+    def start_halo(par):
         for k in range(4):
-            found.append(copy(cs.at[par, pl.ds(k, 1)], hb.at[par, pl.ds(4 * COMPS + k, 1)], hsend.at[par], hrecv.at[par], corner_dev[k]))
-        for k, device in routes:
-            found.append(copy(ws.at[par], hb.at[par, pl.ds(k * COMPS, COMPS)], hsend.at[par], hrecv.at[par], device))
-        return found
+            corner(par, k).start()
+
+        @pl.when(at_bottom)
+        def _():
+            face(par, 1).start()
+        face(par, 0).start()
+
+        @pl.when(jnp.logical_not(at_bottom))
+        def _():
+            face(par, 1).start()
+        face(par, 2).start()
+        face(par, 3).start()
 
     def send_part(par):
         def go(p):
@@ -184,32 +200,85 @@
     for c in range(COMPS):
         ws[0, c] = spack[c]
 
-    pl.semaphore_wait(barrier, len(partners) if near_barrier else n_grp * n_all - 1)
+    if near_barrier:
+        pl.semaphore_wait(barrier, len(partners) + jnp.where(at_bottom, 0, len(above)))
+
+        @pl.when(at_top)
+        def _():
+            for device in above:
+                pl.semaphore_signal(ready, inc=1, device_id=device, device_id_type=pl.DeviceIdType.MESH)
+    else:
+        pl.semaphore_wait(barrier, n_grp * n_all - 1)
 
     half = 2 * MAT
-    to_pair = copy(links_ref, lk.at[pl.ds(g * half, half)], lsend.at[0], lrecv.at[0], (other, zt, xy))
-    to_pair.start()
-
-    def link_faces(h):
-        span = pl.ds(h * MAT, MAT)
+
+    def to_pair(k):
+        found = []
+        for d in range(2):
+            span = d * MAT + k * PAIRS
+            found.append(copy(
+                links_ref.at[pl.ds(span, PAIRS)], lk.at[pl.ds(g * half + span, PAIRS)],
+                lsend.at[k], lrecv.at[k], (other, zt, xy),
+            ))
+        return found
+
+    def span_of(h, k):
+        return pl.ds(h * MAT + k * PAIRS, PAIRS)
+
+    def up_face(h, k):
+        span = span_of(h, k)
+        return copy(sx.at[0, span], xfar.at[0, span], lsend.at[2], lrecv.at[2], (g, zt, x_up))
+
+    def down_face(h, k):
+        span = span_of(h, k)
+        return copy(sx.at[1, span], xfar.at[1, span], lsend.at[2], lrecv.at[2], (g, zt, x_dn))
+
+    def t_copies(h, k):
+        span = span_of(h, k)
         return [
-            copy(sx.at[0, span], xfar.at[0, span], lsend.at[1], lrecv.at[1], (g, zt, x_up)),
-            copy(sx.at[1, span], xfar.at[1, span], lsend.at[1], lrecv.at[1], (g, zt, x_dn)),
-            copy(st.at[0, span], tfar.at[0, span], lsend.at[2], lrecv.at[2], (g, t_up, xy)),
-            copy(st.at[1, span], tfar.at[1, span], lsend.at[2], lrecv.at[2], (g, t_dn, xy)),
+            copy(st.at[0, span], tfar.at[0, span], lsend.at[3], lrecv.at[3], (g, t_up, xy)),
+            copy(st.at[1, span], tfar.at[1, span], lsend.at[3], lrecv.at[3], (g, t_dn, xy)),
         ]
 
-    for item in link_faces(g):
-        item.start()
-    for item in halo(0):
-        item.start()
-
-    to_pair.wait_recv()
-    for c in range(MAT):
-        low, high = lk[other * half + c], lk[other * half + MAT + c]
-        sx[0, pl.ds(other * MAT + c, 1)] = jnp.where(first, roll(low, 4, 0), high)[None]
-        sx[1, pl.ds(other * MAT + c, 1)] = jnp.where(first, low, roll(high, 4, 0))[None]
-        t_faces(other * MAT + c, low, high)
+    def below_near():
+        for k in range(2):
+            down_face(g, k).start()
+        for k in (2, 3):
+            corner(0, k).start()
+        face(0, 1).start()
+
+    for k in range(2):
+        for item in to_pair(k):
+            item.start()
+    for k in range(2):
+        for item in [up_face(g, k)] + t_copies(g, k):
+            item.start()
+    for k in (0, 1):
+        corner(0, k).start()
+    for k in (0, 2, 3):
+        face(0, k).start()
+
+    @pl.when(jnp.logical_not(at_bottom))
+    def _():
+        below_near()
+
+    def pair_part(k):
+        block = lk.at[pl.ds(k * MAT, MAT)]
+        return copy(block, block, lsend.at[k], lrecv.at[k], (other, zt, xy))
+
+    for k in range(2):
+        pair_part(k).wait_recv()
+        for c in range(k * PAIRS, (k + 1) * PAIRS):
+            low, high = lk[other * half + c], lk[other * half + MAT + c]
+            sx[0, pl.ds(other * MAT + c, 1)] = jnp.where(first, roll(low, 4, 0), high)[None]
+            sx[1, pl.ds(other * MAT + c, 1)] = jnp.where(first, low, roll(high, 4, 0))[None]
+            t_faces(other * MAT + c, low, high)
+        for item in [up_face(other, k)] + t_copies(other, k):
+            item.start()
+        if k == 0:
+            @pl.when(jnp.logical_not(at_bottom))
+            def _():
+                down_face(other, 0).start()
     for c in range(PAIRS):
         sx2[c] = jnp.where(first, lk[c], roll(lk[PAIRS + c], 4, 0))
     for c in range(MAT):
@@ -218,13 +287,22 @@
         cs_hl[c:c + 1] = lk[3 * MAT + c][3:4]
         cs_lh[c:c + 1] = lk[c][4:5]
     rest = [
-        copy(sx2, xtwo, lsend.at[3], lrecv.at[3], (g, zt, x_up)),
-        copy(cs_ll, c_ll, lsend.at[4], lrecv.at[4], corner_dev[0]),
-        copy(cs_hl, c_hl, lsend.at[5], lrecv.at[5], corner_dev[2]),
+        copy(sx2, xtwo, lsend.at[4], lrecv.at[4], (g, zt, x_up)),
+        copy(cs_ll, c_ll, lsend.at[5], lrecv.at[5], corner_dev[0]),
         copy(cs_lh, c_lh, lsend.at[6], lrecv.at[6], corner_dev[1]),
+        copy(cs_hl, c_hl, lsend.at[7], lrecv.at[7], corner_dev[2]),
     ]
-    for item in rest + link_faces(other):
+    for item in rest[:3]:
         item.start()
+
+    @pl.when(at_bottom)
+    def _():
+        if near_barrier:
+            pl.semaphore_wait(ready, len(above))
+        below_near()
+        down_face(other, 0).start()
+    down_face(other, 1).start()
+    rest[3].start()
 
     def pick(ref, c):
         return jnp.broadcast_to(ref[c:c + 1], (8, lanes))
@@ -243,14 +321,14 @@
 
     def extend(par, c):
         own_part = ws[par, c]
-        corner = [jnp.broadcast_to(hb[par, 4 * COMPS + k, c:c + 1], (8, lanes)) for k in range(4)]
+        corners = [jnp.broadcast_to(hb[par, 4 * COMPS + k, c:c + 1], (8, lanes)) for k in range(4)]
         x_lo, x_hi, t_lo, t_hi = [hb[par, k * COMPS + c] for k in range(4)]
         return [
             far_rows(x_lo, None, None, 0),
-            far_rows(x_lo, corner[0], corner[1], 1),
+            far_rows(x_lo, corners[0], corners[1], 1),
             widen(c, 0, own_part, t_lo, t_hi),
             widen(c, 1, own_part, t_lo, t_hi),
-            far_rows(x_hi, corner[2], corner[3], 0),
+            far_rows(x_hi, corners[2], corners[3], 0),
             far_rows(x_hi, None, None, 1),
         ]
 
@@ -270,8 +348,9 @@
         for k in range(nshift):
             shiftdirs[k, c] = spack[c]
 
-    copy(st, tfar, lsend.at[2], lrecv.at[2], (g, t_up, xy)).wait()
-    to_pair.wait_send()
+    copy(st, tfar, lsend.at[3], lrecv.at[3], (g, t_up, xy)).wait()
+    for k in range(2):
+        pair_part(k).wait_send()
 
     t_at = lax.rem(zt * cells_t + sub - 2 + n_zt * cells_t, n_zt * cells_t)
     edge = jnp.where(t_at == n_zt * cells_t - 1, -0.5, 0.5)
@@ -335,7 +414,7 @@
                         gauge[2, c, e - 1] = wy + back * roll(turned, NZ, 1)
 
     build((2, 3))
-    for item in [copy(sx, xfar, lsend.at[1], lrecv.at[1], (g, zt, x_up))] + rest:
+    for item in [copy(sx, xfar, lsend.at[2], lrecv.at[2], (g, zt, x_up))] + rest:
         item.wait()
     build((0, 1, 4))
 
@@ -437,8 +516,7 @@
             corner_tiles(packed, par)
             for c in range(COMPS):
                 ws[par, c] = packed[c]
-            for item in halo(par):
-                item.start()
+            start_halo(par)
         catch_up(gain, zeta, beta_shift)
         if not last:
             finish_halo(par)
@@ -520,7 +598,8 @@
             pltpu.VMEM((2, n_all, 1, lanes), f32), pltpu.VMEM((n_all, 1, lanes), f32),
             pltpu.VMEM((9, 16, lanes), f32), rows(16), rows(16), tiles(COMPS), tiles(2 * MAT),
             pltpu.SMEM((nshift,), f32), pltpu.SMEM((nshift,), f32), pltpu.SMEM((1,), f32), dma((5,)),
-            dma((7,)), dma((7,)), dma((2,)), dma((2,)), dma((2,)), dma((2,)), dma((2,)), dma((2,)),
+            dma((8,)), dma((8,)), dma((2,)), dma((2,)), dma((2,)), dma((2,)), dma((2,)), dma((2,)),
+            pltpu.SemaphoreType.REGULAR,
         ],
         compiler_params=pltpu.CompilerParams(collective_id=0, has_side_effects=True),
     )(

time: 60.7 us -> 60.5 us (level)
  no operation moved by 1% of the time
where the time goes in v3:
time: 60.5 us; the launch traced here: 60.3 us
  Pallas kernels  57.9 us (96%)
  between operations  1.8 us (3%)
  local copies, waits for them, and re-layouts  0.61 us (1%)
    pallas_call x1, Pallas kernels, on_device(): pl.pallas_call(functools.partial(kernel, (n_grp, n_zt, n_xy, cells_x, cel...  57.9 us

profile of v3, /device:TPU:0, one launch (start us, length us, event | category | flops | bytes accessed | tf_op | source)
XLA Modules:
  0.0 60.3 jit_solution(9087701239053277743)
XLA Ops:
  1.3 57.9 %shard_map.68 = (f32[6,8,128]{2,1,0:T(8,128)S(1)}, f32[1]{0:T(128)S(4)}) custom-call(f32[6,8,128]{2,1,0:T(8,128)} %bitcast.5, f32[36,8,128]{2,1,0:T(8,128)} %bitcast.4, f32[12]{0:T(128)} %shifts_hbm.1, f32[12]{0:T(128)} %residues_hbm.1, f32[1]{0:T(128)S(6)} %copy.11.mass_hbm), custom_call_target="tpu_custom_call" | custom-call | tf_op jit(solution)/shard_map/pallas_call | solution.py:585
  59.7 0.6 %copy.9 = f32[1,2,3,2,4,128]{5,4,3,2,1,0:T(4,128)} copy(f32[1,2,3,2,4,128]{5,4,3,2,1,0:T(4,128)S(1)} %bitcast.3) | data formatting | bytes 49152

commit v4 on v3

--- a/solution.py
+++ b/solution.py
@@ -131,15 +131,13 @@
 
     def face(par, k):
         device = ((g, zt, x_up), (g, zt, x_dn), (g, t_up, xy), (g, t_dn, xy))[k]
-        return copy(ws.at[par], hb.at[par, pl.ds(k * COMPS, COMPS)], hsend.at[par], hrecv.at[par], device)
+        at = k * COMPS if k < 2 else k * COMPS + 4
+        return copy(ws.at[par], hb.at[par, pl.ds(at, COMPS)], hsend.at[par], hrecv.at[par, k // 2], device)
 
     def corner(par, k):
-        return copy(cs.at[par, pl.ds(k, 1)], hb.at[par, pl.ds(4 * COMPS + k, 1)], hsend.at[par], hrecv.at[par], corner_dev[k])
-
-    def start_halo(par):
-        for k in range(4):
-            corner(par, k).start()
-
+        return copy(cs.at[par, pl.ds(k, 1)], hb.at[par, pl.ds(2 * COMPS + k, 1)], hsend.at[par], hrecv.at[par, 0], corner_dev[k])
+
+    def start_faces(par):
         @pl.when(at_bottom)
         def _():
             face(par, 1).start()
@@ -150,6 +148,10 @@
             face(par, 1).start()
         face(par, 2).start()
         face(par, 3).start()
+
+    def start_corners(par):
+        for k in range(4):
+            corner(par, k).start()
 
     def send_part(par):
         def go(p):
@@ -319,18 +321,18 @@
             row = jnp.where(sub == 6, high_corner, row)
         return row
 
-    def extend(par, c):
-        own_part = ws[par, c]
-        corners = [jnp.broadcast_to(hb[par, 4 * COMPS + k, c:c + 1], (8, lanes)) for k in range(4)]
-        x_lo, x_hi, t_lo, t_hi = [hb[par, k * COMPS + c] for k in range(4)]
-        return [
-            far_rows(x_lo, None, None, 0),
-            far_rows(x_lo, corners[0], corners[1], 1),
-            widen(c, 0, own_part, t_lo, t_hi),
-            widen(c, 1, own_part, t_lo, t_hi),
-            far_rows(x_hi, corners[2], corners[3], 0),
-            far_rows(x_hi, None, None, 1),
-        ]
+    def extend_t(par, c):
+        t_lo, t_hi = hb[par, 2 * COMPS + 4 + c], hb[par, 3 * COMPS + 4 + c]
+        for x in range(2):
+            wide[c, 2 + x] = widen(c, x, ws[par, c], t_lo, t_hi)
+
+    def extend_x(par, c):
+        corners = [jnp.broadcast_to(hb[par, 2 * COMPS + k, c:c + 1], (8, lanes)) for k in range(4)]
+        x_lo, x_hi = hb[par, c], hb[par, COMPS + c]
+        wide[c, 0] = far_rows(x_lo, None, None, 0)
+        wide[c, 1] = far_rows(x_lo, corners[0], corners[1], 1)
+        wide[c, 4] = far_rows(x_hi, corners[2], corners[3], 0)
+        wide[c, 5] = far_rows(x_hi, None, None, 1)
 
     for item in scalars:
         item.wait()
@@ -418,41 +420,56 @@
         item.wait()
     build((0, 1, 4))
 
-    def finish_halo(par):
-        copy(hb.at[par], hb.at[par], hsend.at[par], hrecv.at[par], corner_dev[0]).wait()
-
-    finish_halo(0)
-
-    def hop(field, e0):
-        total = [None] * COMPS
-        terms = (
-            (0, lambda c: field[c, e0 + 1:e0 + 3]),
-            (1, lambda c: field[c, e0 - 1:e0 + 1]),
-            (2, lambda c: roll(field[c, e0:e0 + 2], NZ, 2)),
-            (3, lambda c: z_up(field[c, e0:e0 + 2])),
-            (4, lambda c: z_dn(field[c, e0:e0 + 2])),
-            (5, lambda c: roll(field[c, e0:e0 + 2], -1, 1)),
-            (6, lambda c: roll(field[c, e0:e0 + 2], 1, 1)),
+    def wait_x(par):
+        block = hb.at[par, pl.ds(0, 2 * COMPS + 4)]
+        copy(block, block, hsend.at[par], hrecv.at[par, 0], corner_dev[0]).wait_recv()
+
+    def wait_t(par):
+        block = hb.at[par, pl.ds(2 * COMPS + 4, 2 * COMPS)]
+        copy(block, block, hsend.at[par], hrecv.at[par, 1], corner_dev[0]).wait_recv()
+
+    def wait_sent(par):
+        copy(hb.at[par], hb.at[par], hsend.at[par], hrecv.at[par, 0], corner_dev[0]).wait_send()
+
+    def hop(field, e0, count, terms, total):
+        shifts_of = (
+            lambda c: field[c, e0 + 1:e0 + 1 + count],
+            lambda c: field[c, e0 - 1:e0 - 1 + count],
+            lambda c: roll(field[c, e0:e0 + count], NZ, 2),
+            lambda c: z_up(field[c, e0:e0 + count]),
+            lambda c: z_dn(field[c, e0:e0 + count]),
+            lambda c: roll(field[c, e0:e0 + count], -1, 1),
+            lambda c: roll(field[c, e0:e0 + count], 1, 1),
         )
-        for term, shifted in terms:
-            v = [shifted(c) for c in range(COMPS)]
+        for term in terms:
+            v = [shifts_of[term](c) for c in range(COMPS)]
             for i in range(3):
                 for j in range(3):
-                    wre = gauge[term, i * 3 + j, e0 - 1:e0 + 1]
-                    wim = gauge[term, PAIRS + i * 3 + j, e0 - 1:e0 + 1]
+                    wre = gauge[term, i * 3 + j, e0 - 1:e0 - 1 + count]
+                    wim = gauge[term, PAIRS + i * 3 + j, e0 - 1:e0 - 1 + count]
                     re = wre * v[j] - wim * v[3 + j]
                     im = wre * v[3 + j] + wim * v[j]
                     total[i] = re if total[i] is None else total[i] + re
                     total[3 + i] = im if total[3 + i] is None else total[3 + i] + im
         return total
 
+    every = tuple(range(7))
+
     def hop_wide(par):
+        wait_t(par)
         for c in range(COMPS):
-            for e, value in enumerate(extend(par, c)):
-                wide[c, e] = value
-        for e0 in (1, 3):
-            for c, value in enumerate(hop(wide, e0)):
-                hop_w[c, e0:e0 + 2] = value
+            extend_t(par, c)
+        for c, value in enumerate(hop(wide, 2, 2, every[2:], [None] * COMPS)):
+            hop_w[c, 2:4] = value
+        wait_x(par)
+        for c in range(COMPS):
+            extend_x(par, c)
+        for c, value in enumerate(hop(wide, 2, 2, every[:2], [hop_w[c, 2:4] for c in range(COMPS)])):
+            hop_w[c, 2:4] = value
+        for e in (1, 4):
+            for c, value in enumerate(hop(wide, e, 1, every, [None] * COMPS)):
+                hop_w[c, e:e + 1] = value
+        wait_sent(par)
 
     hop_wide(0)
     for c in range(COMPS):
@@ -461,7 +478,7 @@
         mid[c, 1:5] = hop_w[c, 1:5]
 
     def image_of():
-        image = hop(mid, 2)
+        image = hop(mid, 2, 2, every, [None] * COMPS)
         packed = []
         for c in range(COMPS):
             wp = jnp.where(first, roll(image[c][0], -2, 0), roll(image[c][1], 2, 0))
@@ -507,19 +524,20 @@
             mine[...] = packed_state
             swap.start()
         packed, dpack = image_of()
+        if not last:
+            corner_tiles(packed, par)
+            start_corners(par)
+            for c in range(COMPS):
+                ws[par, c] = packed[c]
         res = [rpack[c] for c in range(COMPS)]
         part[par, pl.ds(me, 1)] = dots([inner(dpack, packed), inner(res, packed), inner(packed, packed), inner(spack, res)])[None]
         send_part(par)
         if last:
             send_cross(par)
         else:
-            corner_tiles(packed, par)
-            for c in range(COMPS):
-                ws[par, c] = packed[c]
-            start_halo(par)
+            start_faces(par)
         catch_up(gain, zeta, beta_shift)
         if not last:
-            finish_halo(par)
             hop_wide(par)
         wait_part(par)
         sums = summed(lambda j: part[par, j])
@@ -598,7 +616,7 @@
             pltpu.VMEM((2, n_all, 1, lanes), f32), pltpu.VMEM((n_all, 1, lanes), f32),
             pltpu.VMEM((9, 16, lanes), f32), rows(16), rows(16), tiles(COMPS), tiles(2 * MAT),
             pltpu.SMEM((nshift,), f32), pltpu.SMEM((nshift,), f32), pltpu.SMEM((1,), f32), dma((5,)),
-            dma((8,)), dma((8,)), dma((2,)), dma((2,)), dma((2,)), dma((2,)), dma((2,)), dma((2,)),
+            dma((8,)), dma((8,)), dma((2,)), dma((2, 2)), dma((2,)), dma((2,)), dma((2,)), dma((2,)),
             pltpu.SemaphoreType.REGULAR,
         ],
         compiler_params=pltpu.CompilerParams(collective_id=0, has_side_effects=True),

time: 60.5 us -> 58.6 us (0.969)
  Pallas kernels: 57.9 us -> 56 us
    pallas_call x1, Pallas kernels: 57.9 us -> 56 us  [on_device(): pl.pallas_call(functools.partial(kernel, (n_grp, n_zt, n_xy, cells_x, cel...]
where the time goes in v4:
time: 58.6 us; the launch traced here: 58.4 us
  Pallas kernels  56 us (96%)
  between operations  1.8 us (3%)
  local copies, waits for them, and re-layouts  0.61 us (1%)
    pallas_call x1, Pallas kernels, on_device(): pl.pallas_call(functools.partial(kernel, (n_grp, n_zt, n_xy, cells_x, cel...  56 us

profile of v4, /device:TPU:0, one launch (start us, length us, event | category | flops | bytes accessed | tf_op | source)
XLA Modules:
  0.0 58.4 jit_solution(10611308494538728631)
XLA Ops:
  1.3 56.0 %shard_map.68 = (f32[6,8,128]{2,1,0:T(8,128)S(1)}, f32[1]{0:T(128)S(4)}) custom-call(f32[6,8,128]{2,1,0:T(8,128)} %bitcast.5, f32[36,8,128]{2,1,0:T(8,128)} %bitcast.4, f32[12]{0:T(128)} %shifts_hbm.1, f32[12]{0:T(128)} %residues_hbm.1, f32[1]{0:T(128)S(6)} %copy.11.mass_hbm), custom_call_target="tpu_custom_call" | custom-call | tf_op jit(solution)/shard_map/pallas_call | solution.py:603
  57.8 0.6 %copy.9 = f32[1,2,3,2,4,128]{5,4,3,2,1,0:T(4,128)} copy(f32[1,2,3,2,4,128]{5,4,3,2,1,0:T(4,128)S(1)} %bitcast.3) | data formatting | bytes 49152

commit v5 on v4

--- a/solution.py
+++ b/solution.py
@@ -138,6 +138,9 @@
         return copy(cs.at[par, pl.ds(k, 1)], hb.at[par, pl.ds(2 * COMPS + k, 1)], hsend.at[par], hrecv.at[par, 0], corner_dev[k])
 
     def start_faces(par):
+        face(par, 2).start()
+        face(par, 3).start()
+
         @pl.when(at_bottom)
         def _():
             face(par, 1).start()
@@ -146,8 +149,6 @@
         @pl.when(jnp.logical_not(at_bottom))
         def _():
             face(par, 1).start()
-        face(par, 2).start()
-        face(par, 3).start()
 
     def start_corners(par):
         for k in range(4):
@@ -524,13 +525,14 @@
             mine[...] = packed_state
             swap.start()
         packed, dpack = image_of()
+        res = [rpack[c] for c in range(COMPS)]
+        sums_row = dots([inner(dpack, packed), inner(res, packed), inner(packed, packed), inner(spack, res)])
         if not last:
             corner_tiles(packed, par)
-            start_corners(par)
             for c in range(COMPS):
                 ws[par, c] = packed[c]
-        res = [rpack[c] for c in range(COMPS)]
-        part[par, pl.ds(me, 1)] = dots([inner(dpack, packed), inner(res, packed), inner(packed, packed), inner(spack, res)])[None]
+            start_corners(par)
+        part[par, pl.ds(me, 1)] = sums_row[None]
         send_part(par)
         if last:
             send_cross(par)

time: 58.6 us -> 58.6 us (level)
  no operation moved by 1% of the time
where the time goes in v5:
time: 58.6 us; the launch traced here: 58.4 us
  Pallas kernels  56 us (96%)
  between operations  1.8 us (3%)
  local copies, waits for them, and re-layouts  0.61 us (1%)
    pallas_call x1, Pallas kernels, on_device(): pl.pallas_call(functools.partial(kernel, (n_grp, n_zt, n_xy, cells_x, cel...  56 us

profile of v5, /device:TPU:0, one launch (start us, length us, event | category | flops | bytes accessed | tf_op | source)
XLA Modules:
  0.0 58.4 jit_solution(10889398184381998531)
XLA Ops:
  1.3 56.0 %shard_map.68 = (f32[6,8,128]{2,1,0:T(8,128)S(1)}, f32[1]{0:T(128)S(4)}) custom-call(f32[6,8,128]{2,1,0:T(8,128)} %bitcast.5, f32[36,8,128]{2,1,0:T(8,128)} %bitcast.4, f32[12]{0:T(128)} %shifts_hbm.1, f32[12]{0:T(128)} %residues_hbm.1, f32[1]{0:T(128)S(6)} %copy.11.mass_hbm), custom_call_target="tpu_custom_call" | custom-call | tf_op jit(solution)/shard_map/pallas_call | solution.py:605
  57.8 0.6 %copy.9 = f32[1,2,3,2,4,128]{5,4,3,2,1,0:T(4,128)} copy(f32[1,2,3,2,4,128]{5,4,3,2,1,0:T(4,128)S(1)} %bitcast.3) | data formatting | bytes 49152
